TPU v7x, 32 devices: a whole 2x2x4 slice. The times are simulated.
32 devices in a mesh: virt: 8 (over z, x), aux: 4 (over y, core).
Axes of the slice: x: 2, y: 2, z: 4, core: 2. Of those that a mesh axis runs over, the one named last changes fastest.
Arguments:
- three_index: bfloat16 [600, 5120], P('aux', 'virt'), may hold values from -0.0625 to 0.0625
- eps_occ: float32 [20], replicated, may hold values from -1.5 to -0.5
- eps_virt: float32 [256], replicated, may hold values from 0.3 to 3
Outputs:
- virt_energy: float32 [256], P('virt')
- pair_energy: float32 [20, 20], replicated
All inputs are finite; a program needn't handle non-finite values.
Results may differ from a plain program's by a relative error of at most 0.0003.
Values may be sent and summed in bfloat16 or wider, within the bound.
A program may use at most 128 MiB of HBM per device.

v0:
```python
import jax
import jax.numpy as jnp
from jax import lax
from jax.sharding import PartitionSpec as P


def on_device(three_index, eps_occ, eps_virt):
    occupied = eps_occ.shape[0]
    own_width = three_index.shape[1] // occupied
    virt_count = lax.axis_size("virt")
    aux_place = lax.axis_index("aux")
    virt_place = lax.axis_index("virt")
    narrow = lax.all_to_all(three_index, "aux", split_axis=1, concat_axis=0, tiled=True)
    partner = lax.all_gather(narrow, "virt", axis=1, tiled=True)
    stride = narrow.shape[1] // occupied
    table = eps_virt.reshape(virt_count, own_width)
    eps_other = lax.dynamic_slice_in_dim(table, aux_place * stride, stride, 1).reshape(-1)
    other_width = partner.shape[1] // occupied
    partner_cube = partner.reshape(partner.shape[0], other_width, occupied)
    eps_own = lax.dynamic_slice_in_dim(eps_virt, virt_place * own_width, own_width)
    incoming = lax.all_gather(three_index, "aux", axis=0, tiled=True)
    rows = incoming.shape[0]
    left_cube = incoming.reshape(rows, own_width, occupied)
    integrals = jnp.einsum(
        "pai,pbj->iajb", left_cube, partner_cube, preferred_element_type=jnp.float32
    )
    denominator = (
        eps_occ[:, None, None, None]
        + eps_occ[None, None, :, None]
        - eps_own[None, :, None, None]
        - eps_other[None, None, None, :]
    )
    swapped = jnp.transpose(integrals, (2, 1, 0, 3))
    energy_terms = integrals * (2.0 * integrals - swapped) / denominator
    virt_local = jnp.sum(energy_terms, axis=(0, 2, 3))
    pair_local = jnp.sum(energy_terms, axis=(1, 3))
    virt_energy, pair_column = lax.psum((virt_local, pair_local), "aux")
    pair_energy = lax.psum(pair_column, "virt")
    return (virt_energy, pair_energy)


def solution(mesh):
    in_specs = (P("aux", "virt"), P(), P())
    out_specs = (P("virt"), P())
    return jax.shard_map(
        on_device, mesh=mesh, in_specs=in_specs, out_specs=out_specs, check_vma=False
    )
```

profile of v0, /device:TPU:0, one launch (start us, length us, event | category | flops | bytes accessed | tf_op | source)
XLA Modules:
  0.0 129.4 jit_solution(3256470533484505875)
XLA Ops:
  7.2 0.0 copy-start
  7.2 0.0 all-gather.3.cloned.1.call-start
  7.2 1.2 all_to_all.14
  8.4 10.6 %all_to_all.19 = bf16[150,4,160]{2,0,1:T(8,128)(2,1)S(1)} all-to-all(bf16[150,4,160]{2,0,1:T(8,128)(2,1)S(1)} %copy.16), channel_id=1, replica_groups=mesh['virt'=8,'aux'=4] {'aux'}, dimensions={1} | all-to-all | bytes 384000 | tf_op jit(solution)/shard_map/all_to_all | solution.py:13
  19.0 0.1 reshape.63
  19.1 0.8 copy.23
  20.0 0.0 all-gather.3.cloned.1.call-update
  20.0 0.8 reshape.57
  20.8 0.8 dynamic_slice.6
  21.5 0.1 constant_dynamic-slice_fusion
  21.6 0.1 sub.41
  21.7 8.4 %all-gather = bf16[4,150,640]{2,1,0:T(8,128)(2,1)S(1)} all-gather(bf16[1,150,640]{2,1,0:T(8,128)(2,1)} %bitcast.31), channel_id=1, replica_groups=mesh['virt'=8,'aux'=4] {'aux'}, dimensions={0}, use_global_device_ids=true | all-gather | bytes 960000 | tf_op jit(solution)/shard_map/all_gather | solution.py:21
  30.0 1.2 copy.18
  31.3 1.1 reshape.56
  32.4 0.0 copy-done
  32.4 0.1 broadcast_add_fusion
  32.5 0.1 broadcast_subtract_fusion
  32.6 32.6 %all-gather.3.cloned.1.call-done = bf16[600,1280]{0,1:T(8,128)(2,1)} async-done(((bf16[600,160]{0,1:T(8,128)(2,1)}), bf16[600,1280]{0,1:T(8,128)(2,1)}) %all-gather.3.cloned.1.call-update) | async-done | bytes 1536016 | tf_op jit(solution)/shard_map/all_gather | solution.py:14
  65.3 2.7 %reshape.55 = bf16[600,64,20]{0,2,1:T(8,128)(2,1)S(1)} reshape(bf16[600,1280]{0,1:T(8,128)(2,1)} %all-gather.3.cloned.1.call-done) | data formatting | bytes 3072000 | tf_op jit(solution)/shard_map/reshape | solution.py:19
  67.9 2.7 %fusion.2 = f32[64,20,32,20]{0,2,3,1:T(8,128)S(1)} fusion(bf16[600,64,20,1]{0,2,1,3:T(8,128)(2,1)S(1)} %bitcast.29, bf16[600,32,20]{0,2,1:T(8,128)(2,1)S(1)} %reshape.56), kind=kOutput, calls=%fused_computation.4 | convolution fusion | flops 983040000 | bytes 5580800 | tf_op jit(solution)/shard_map/pai,pbj->iajb/dot_general | solution.py:24
  70.7 6.5 %fusion.6 = (f32[20,20]{1,0:T(8,128)S(1)}, f32[32]{0:T(128)S(1)}) fusion(f32[64]{0:T(128)S(1)} %sub.41, f32[20,32,20]{1,2,0:T(8,128)S(1)} %broadcast_subtract_fusion, f32[64,20,32,20]{0,2,3,1:T(8,128)S(1)} %fusion.2), kind=kLoop, calls=%fused_computation.8 | loop fusion | flops 5733968 | bytes 3329984 | tf_op jit(solution)/shard_map/reduce_sum | solution.py:36
  77.2 10.6 %all-reduce = (f32[32]{0:T(128)}, f32[20,20]{1,0:T(8,128)S(1)}) all-reduce(f32[32]{0:T(128)S(1)} %get-tuple-element.3, f32[20,20]{1,0:T(8,128)S(1)} %get-tuple-element.2), channel_id=1, replica_groups=mesh['virt'=8,'aux'=4] {'aux'}, use_global_device_ids=true, to_apply=%region_1.0 | all-reduce | flops 432 | bytes 3456 | tf_op jit(solution)/shard_map/psum | solution.py:37
  87.8 34.8 %psum.23 = f32[20,20]{1,0:T(8,128)} all-reduce(f32[20,20]{1,0:T(8,128)S(1)} %get-tuple-element.5), channel_id=1, replica_groups=mesh['virt'=8,'aux'=4] {'virt'}, use_global_device_ids=true, to_apply=%region_4.0 | all-reduce | flops 400 | bytes 3200 | tf_op jit(solution)/shard_map/psum | solution.py:38
  (1 shorter events, 0.0 us)
Async XLA Ops:
  7.2 25.2 %copy-start = (f32[20]{0:T(128)S(1)}, f32[20]{0:T(128)}, u32[]{:S(2)}) copy-start(f32[20]{0:T(128)} %param.4) | copy-start | bytes 244
  7.2 58.1 %all-gather.3.cloned.1.call-start = ((), (), s32[]{:S(2)}) async-start(), calls=%async_computation.1 | async-start | bytes 1843200 | tf_op jit(solution)/shard_map/all_gather | solution.py:14
Sparse Core Ops, SparseCore 0:
  20.1 45.0 all-gather.2
where the time goes:
time: 130 us; the launch traced here: 129 us
  blocking collectives  64.4 us (50%)
  waiting for transfers between devices  32.7 us (25%)
  between operations  14.1 us (11%)
  local copies, waits for them, and re-layouts  8.83 us (7%)
  other arithmetic  6.69 us (5%)
  matrix products  2.73 us (2%)
    psum x1, blocking collectives, on_device(): pair_energy = lax.psum(pair_column, 'virt')  34.8 us
    all_gather x1, waiting for transfers between devices, on_device(): partner = lax.all_gather(narrow, 'virt', axis=1, tiled=True)  32.6 us
    psum x1, blocking collectives, on_device(): virt_energy, pair_column = lax.psum((virt_local, pair_local), 'aux')  10.6 us
    all_to_all x1, blocking collectives, on_device(): lax.all_to_all(three_index, 'aux', split_axis=1, concat_axis=0, tiled=True)  10.6 us
    all_gather x1, blocking collectives, on_device(): incoming = lax.all_gather(three_index, 'aux', axis=0, tiled=True)  8.36 us
    reduce_sum x1, other arithmetic, on_device(): pair_local = jnp.sum(energy_terms, axis=(1, 3))  6.49 us
    dot_general x1, matrix products, on_device(): jnp.einsum('pai,pbj->iajb', left_cube, partner_cube, preferred_element_ty...  2.73 us
    reshape x1, local copies, waits for them, and re-layouts, on_device(): partner_cube = partner.reshape(partner.shape[0], other_width, occupied)  2.67 us
  transfers between devices with their start and end apart: 1, of which 1 were waited for; matrix products, arithmetic and copies ran while one was open for 3% of the time, Pallas kernels for 0%

commit v1 on v0

--- a/solution.py
+++ b/solution.py
@@ -35,7 +35,8 @@
     virt_local = jnp.sum(energy_terms, axis=(0, 2, 3))
     pair_local = jnp.sum(energy_terms, axis=(1, 3))
     virt_energy, pair_column = lax.psum((virt_local, pair_local), "aux")
-    pair_energy = lax.psum(pair_column, "virt")
+    pieces = lax.all_gather(pair_column, "virt")
+    pair_energy = jnp.sum(pieces, axis=0)
     return (virt_energy, pair_energy)
 
 

time: 130 us -> 126 us (0.969)
  blocking collectives: 64.4 us -> 60.1 us
    psum x1 -> x0, blocking collectives: 34.8 us -> none  [on_device(): pair_energy = lax.psum(pair_column, 'virt')]
    all_gather x0 -> x1, blocking collectives: none -> 30.5 us  [on_device(): pieces = lax.all_gather(pair_column, 'virt')]
where the time goes in v1:
time: 126 us
  blocking collectives  60.1 us (48%)
  waiting for transfers between devices  32.7 us (26%)
  between operations  14.1 us (11%)
  local copies, waits for them, and re-layouts  8.83 us (7%)
  other arithmetic  7.3 us (6%)
  matrix products  2.73 us (2%)
    all_gather x1, waiting for transfers between devices, on_device(): partner = lax.all_gather(narrow, 'virt', axis=1, tiled=True)  32.6 us
    all_gather x1, blocking collectives, on_device(): pieces = lax.all_gather(pair_column, 'virt')  30.5 us
    psum x1, blocking collectives, on_device(): virt_energy, pair_column = lax.psum((virt_local, pair_local), 'aux')  10.6 us
    all_to_all x1, blocking collectives, on_device(): lax.all_to_all(three_index, 'aux', split_axis=1, concat_axis=0, tiled=True)  10.6 us
    all_gather x1, blocking collectives, on_device(): incoming = lax.all_gather(three_index, 'aux', axis=0, tiled=True)  8.36 us
    reduce_sum x1, other arithmetic, on_device(): pair_local = jnp.sum(energy_terms, axis=(1, 3))  6.49 us
    dot_general x1, matrix products, on_device(): jnp.einsum('pai,pbj->iajb', left_cube, partner_cube, preferred_element_ty...  2.73 us
    reshape x1, local copies, waits for them, and re-layouts, on_device(): partner_cube = partner.reshape(partner.shape[0], other_width, occupied)  2.67 us
  transfers between devices with their start and end apart: 1, of which 1 were waited for; matrix products, arithmetic and copies ran while one was open for 3% of the time, Pallas kernels for 0%

profile of v1, /device:TPU:0, one launch (start us, length us, event | category | flops | bytes accessed | tf_op | source)
XLA Modules:
  0.0 125.8 jit_solution(13522278502170953506)
XLA Ops:
  7.2 0.0 copy-start
  7.2 0.0 all-gather.3.cloned.1.call-start
  7.2 1.2 all_to_all.14
  8.4 10.6 %all_to_all.19 = bf16[150,4,160]{2,0,1:T(8,128)(2,1)S(1)} all-to-all(bf16[150,4,160]{2,0,1:T(8,128)(2,1)S(1)} %copy.16), channel_id=1, replica_groups=mesh['virt'=8,'aux'=4] {'aux'}, dimensions={1} | all-to-all | bytes 384000 | tf_op jit(solution)/shard_map/all_to_all | solution.py:13
  19.0 0.1 reshape.63
  19.1 0.8 copy.23
  20.0 0.0 all-gather.3.cloned.1.call-update
  20.0 0.8 reshape.57
  20.8 0.8 dynamic_slice.6
  21.5 0.1 constant_dynamic-slice_fusion
  21.6 0.1 sub.41
  21.7 8.4 %all-gather = bf16[4,150,640]{2,1,0:T(8,128)(2,1)S(1)} all-gather(bf16[1,150,640]{2,1,0:T(8,128)(2,1)} %bitcast.32), channel_id=1, replica_groups=mesh['virt'=8,'aux'=4] {'aux'}, dimensions={0}, use_global_device_ids=true | all-gather | bytes 960000 | tf_op jit(solution)/shard_map/all_gather | solution.py:21
  30.0 1.2 copy.18
  31.3 1.1 reshape.56
  32.4 0.0 copy-done
  32.4 0.1 broadcast_add_fusion
  32.5 0.1 broadcast_subtract_fusion
  32.6 32.6 %all-gather.3.cloned.1.call-done = bf16[600,1280]{0,1:T(8,128)(2,1)} async-done(((bf16[600,160]{0,1:T(8,128)(2,1)}), bf16[600,1280]{0,1:T(8,128)(2,1)}) %all-gather.3.cloned.1.call-update) | async-done | bytes 1536016 | tf_op jit(solution)/shard_map/all_gather | solution.py:14
  65.3 2.7 %reshape.55 = bf16[600,64,20]{0,2,1:T(8,128)(2,1)S(1)} reshape(bf16[600,1280]{0,1:T(8,128)(2,1)} %all-gather.3.cloned.1.call-done) | data formatting | bytes 3072000 | tf_op jit(solution)/shard_map/reshape | solution.py:19
  67.9 2.7 %fusion.2 = f32[64,20,32,20]{0,2,3,1:T(8,128)S(1)} fusion(bf16[600,64,20,1]{0,2,1,3:T(8,128)(2,1)S(1)} %bitcast.30, bf16[600,32,20]{0,2,1:T(8,128)(2,1)S(1)} %reshape.56), kind=kOutput, calls=%fused_computation.4 | convolution fusion | flops 983040000 | bytes 5580800 | tf_op jit(solution)/shard_map/pai,pbj->iajb/dot_general | solution.py:24
  70.7 6.5 %fusion.6 = (f32[20,20]{1,0:T(8,128)S(1)}, f32[32]{0:T(128)S(1)}) fusion(f32[64]{0:T(128)S(1)} %sub.41, f32[20,32,20]{1,2,0:T(8,128)S(1)} %broadcast_subtract_fusion, f32[64,20,32,20]{0,2,3,1:T(8,128)S(1)} %fusion.2), kind=kLoop, calls=%fused_computation.8 | loop fusion | flops 5733968 | bytes 3329984 | tf_op jit(solution)/shard_map/reduce_sum | solution.py:36
  77.2 10.6 %all-reduce = (f32[32]{0:T(128)}, f32[1,20,20]{2,1,0:T(8,128)S(1)}) all-reduce(f32[32]{0:T(128)S(1)} %get-tuple-element.3, f32[1,20,20]{2,1,0:T(8,128)S(1)} %bitcast.33), channel_id=1, replica_groups=mesh['virt'=8,'aux'=4] {'aux'}, use_global_device_ids=true, to_apply=%region_1.0 | all-reduce | flops 432 | bytes 3456 | tf_op jit(solution)/shard_map/psum | solution.py:37
  87.8 30.5 %all_gather.15 = f32[8,20,20]{2,1,0:T(8,128)S(1)} all-gather(f32[1,20,20]{2,1,0:T(8,128)S(1)} %get-tuple-element.5), channel_id=1, replica_groups=mesh['virt'=8,'aux'=4] {'virt'}, dimensions={0}, use_global_device_ids=true | all-gather | bytes 14400 | tf_op jit(solution)/shard_map/all_gather | solution.py:38
  118.4 0.6 reduce_sum.29
  (1 shorter events, 0.0 us)
Async XLA Ops:
  7.2 25.2 %copy-start = (f32[20]{0:T(128)S(1)}, f32[20]{0:T(128)}, u32[]{:S(2)}) copy-start(f32[20]{0:T(128)} %param.4) | copy-start | bytes 244
  7.2 58.1 %all-gather.3.cloned.1.call-start = ((), (), s32[]{:S(2)}) async-start(), calls=%async_computation.1 | async-start | bytes 1843200 | tf_op jit(solution)/shard_map/all_gather | solution.py:14
Sparse Core Ops, SparseCore 0:
  20.1 45.0 all-gather.2
